TPU v7x, 32 devices: a whole 2x2x4 slice. The times are simulated.
32 devices in a mesh: expert: 8 (over z, y), gate: 4 (over x, core).
Axes of the slice: x: 2, y: 2, z: 4, core: 2. Of those that a mesh axis runs over, the one named last changes fastest.
Arguments:
- samples: bfloat16 [6144, 4096], P('expert', 'gate'), may hold values from -4 to 4
- gate_weight: bfloat16 [4096, 32], P('gate'), may hold values from -1 to 1
- expert_ids: int32 [6144, 2], P('expert'), may hold values from 0 to 31, all different within a row; in each aligned block of 768 rows (0 to 767, 768 to 1535, ...) at most 96 rows name the same one
- pad_mask: int32 [6144], P('expert'), may hold values 0 or 1
- up_weight: bfloat16 [32, 4096, 1024], P(('expert', 'gate')), may hold values from -0.09375 to 0.09375
- down_weight: bfloat16 [32, 1024, 1024], P(('expert', 'gate')), may hold values from -0.1875 to 0.1875
Outputs:
- combined: bfloat16 [6144, 1024], P('expert', 'gate')
Inputs may be any that keep to these rules, and one draw needn't show every extreme that they name: `expert_ids`: each sample names two different experts; among the 768 samples of one index of expert no expert is named more than 96 times, a bound that some block reaches.
All inputs are finite; a program needn't handle non-finite values. No bound on the sum of `pad_mask` on one device may be relied on, other than what follows from the above.
Results may differ from a plain program's by a relative error of at most 0.0057.
Values may be sent and summed in bfloat16 or wider, within the bound.
A program may use at most 128 MiB of HBM per device.

v0:
```python
import jax
import jax.numpy as jnp
from jax import lax
from jax.sharding import PartitionSpec as P


def joined(shard, axis, combine):
    everything = jax.tree.map(lambda part: lax.all_gather(part, axis), shard)
    leading = jax.tree.map(lambda part: part[0], everything)

    def step(k, so_far):
        return combine(so_far, jax.tree.map(lambda part: part[k], everything))

    return lax.fori_loop(1, lax.axis_size(axis), step, leading)


def combine_parts(first, second):
    row_top = jnp.maximum(first[0], second[0])
    left_scale = jnp.exp(first[0] - row_top)
    right_scale = jnp.exp(second[0] - row_top)
    row_total = first[1] * left_scale + second[1] * right_scale
    chosen = first[2] * left_scale[None, :] + second[2] * right_scale[None, :]
    return (row_top, row_total, chosen)


def per_device(samples, gate_weight, expert_ids, pad_mask, up_weight, down_weight):
    row_count = samples.shape[0]
    group_count = lax.axis_size("expert")
    gate_count = lax.axis_size("gate")
    expert_count = group_count * gate_count
    capacity = 4 * row_count // expert_count
    col_count = expert_count // gate_count
    gate_index = lax.axis_index("gate")
    logits_t = lax.psum_scatter(
        lax.dot_general(
            gate_weight, samples, (((0,), (1,)), ((), ())), preferred_element_type=jnp.float32
        ),
        "gate",
        scatter_dimension=0,
        tiled=True,
    )
    flat_ids = expert_ids.reshape(-1)
    onehot = (flat_ids[:, None] == jnp.arange(expert_count, dtype=jnp.int32)[None, :]).astype(
        jnp.int32
    )
    slot_rank = jnp.sum(onehot * (jnp.cumsum(onehot, axis=0) - 1), axis=1)
    position = flat_ids * capacity + slot_rank
    row_index = jnp.repeat(jnp.arange(row_count, dtype=jnp.int32), 2)
    owners = jnp.full((expert_count * capacity,), row_count, jnp.int32).at[position].set(row_index)
    whole_rows = lax.all_gather(samples, "gate", axis=1, tiled=True)
    padded = jnp.concatenate(
        [whole_rows, jnp.zeros((1, whole_rows.shape[1]), whole_rows.dtype)], axis=0
    )
    column_owners = lax.dynamic_index_in_dim(
        owners.reshape(group_count, gate_count, capacity), gate_index, 1, keepdims=False
    )
    outgoing = padded[column_owners]
    incoming = lax.all_to_all(outgoing, "expert", split_axis=0, concat_axis=0, tiled=True)
    slot_rows = incoming.reshape(group_count * capacity, whole_rows.shape[1])
    hidden = jnp.dot(slot_rows, up_weight[0], preferred_element_type=jnp.float32)
    active = jnp.maximum(hidden, 0.0).astype(jnp.bfloat16)
    expert_out = jnp.dot(active, down_weight[0], preferred_element_type=jnp.float32).astype(
        jnp.bfloat16
    )
    out_share = expert_out.shape[1] // gate_count
    outbound = expert_out.reshape(group_count, 1, 1, capacity, gate_count, out_share)
    returned = lax.all_to_all(
        lax.all_to_all(outbound, "expert", split_axis=0, concat_axis=1, tiled=True),
        "gate",
        split_axis=4,
        concat_axis=2,
        tiled=True,
    )
    returned = returned.reshape(expert_count * capacity, out_share)
    offset = expert_ids - gate_index * col_count
    inside = ((offset >= 0) & (offset < col_count)).T
    chosen = jnp.take_along_axis(logits_t, jnp.clip(offset, 0, col_count - 1).T, axis=0)
    local_top = jnp.max(logits_t, axis=0)
    local_total = jnp.sum(jnp.exp(logits_t - local_top[None, :]), axis=0)
    local_chosen = jnp.where(inside, jnp.exp(chosen - local_top[None, :]), 0.0)
    row_top, row_total, numerator = joined(
        (local_top, local_total, local_chosen), "gate", combine_parts
    )
    factor = expert_count * numerator / row_total[None, :] * pad_mask.astype(jnp.float32)[None, :]
    picked = returned[position].astype(jnp.float32).reshape(row_count, 2, out_share)
    mixed = factor[0][:, None] * picked[:, 0, :] + factor[1][:, None] * picked[:, 1, :]
    return mixed.astype(jnp.bfloat16)


def solution(mesh):
    placed = (
        P("expert", "gate"),
        P("gate", None),
        P("expert", None),
        P("expert"),
        P(("expert", "gate"), None, None),
        P(("expert", "gate"), None, None),
    )
    return jax.shard_map(
        per_device, mesh=mesh, in_specs=placed, out_specs=P("expert", "gate"), check_vma=False
    )
```

profile of v0, /device:TPU:0, one launch (start us, length us, event | category | flops | bytes accessed | tf_op | source)
XLA Modules:
  0.0 345.1 jit_solution(15891063067835120710)
XLA Ops:
  6.5 0.0 all-gather.8.cloned.1.call-start
  6.5 0.7 all-gather.8.cloned.1.call-update
  7.3 0.9 copy.19
  8.1 0.2 eq.29
  8.4 0.2 eq.25
  8.6 0.7 broadcast_multiply_fusion
  9.3 0.2 copy.18
  9.5 0.3 mul.137
  9.8 9.1 %reduce-window.6 = s32[32,12,128]{2,1,0:T(8,128)S(1)} reduce-window(s32[32,12,128]{2,1,0:T(8,128)S(1)} %fusion.14, s32[]{:T(128)} %constant.77.clone.1), window={size=1x1x128 pad=0_0x0_0x127_0}, to_apply=%region_5.6 | reduce-window | flops 6242304 | bytes 393220 | tf_op jit(solution)/shard_map/reduce-window
  18.8 0.1 slice.52
  19.0 0.2 copy.21
  19.2 0.1 copy.22
  19.3 0.2 reshape.149
  19.6 0.1 add_add_fusion
  19.7 0.1 fusion.16
  19.8 6.2 %scatter_custom_fusion = s32[3072]{0:T(1024)S(1)} fusion(s32[1536]{0:T(1024)S(1)} %fusion.17, s32[1536]{0:T(1024)S(1)} %reshape.149, s32[]{:T(128)} %constant.86.clone.1), kind=kCustom, calls=%fused_computation.44 | custom fusion | bytes 12292 | tf_op jit(solution)/shard_map/scatter | solution.py:49
  26.0 0.1 reshape.118
  26.1 0.1 reshape.125
  26.2 31.8 %all-gather.8.cloned.1.call-done = bf16[768,4096]{1,0:T(8,128)(2,1)} async-done(((bf16[768,1024]{1,0:T(8,128)(2,1)}), bf16[768,4096]{1,0:T(8,128)(2,1)}) %all-gather.8.cloned.1.call-update) | async-done | bytes 6291472 | tf_op jit(solution)/shard_map/all_gather | solution.py:50
  58.0 6.2 %concatenate.3 = bf16[769,4096]{1,0:T(8,128)(2,1)} pad(bf16[768,4096]{1,0:T(8,128)(2,1)} %all-gather.8.cloned.1.call-done, bf16[]{:T(256)} %constant.85.clone.1), padding=0_1x0_0 | pad | bytes 12591106 | tf_op jit(solution)/shard_map/concatenate | solution.py:51
  64.3 15.6 %gather_fusion = bf16[768,4096]{1,0:T(8,128)(2,1)} fusion(bf16[769,4096]{1,0:T(8,128)(2,1)} %concatenate.3, s32[1024]{0:T(1024)S(1)} %pad_clamp_fusion.1), kind=kCustom, calls=%fused_computation | custom fusion | bytes 12585984 | tf_op jit(solution)/shard_map/gather | solution.py:57
  79.8 144.1 %all_to_all.32 = bf16[8,96,4096]{2,1,0:T(8,128)(2,1)} all-to-all(bf16[8,96,4096]{2,1,0:T(8,128)(2,1)} %bitcast.93), channel_id=1, replica_groups=mesh['expert'=8,'gate'=4] {'expert'}, dimensions={0} | all-to-all | bytes 12582912 | tf_op jit(solution)/shard_map/all_to_all | solution.py:58
  223.9 0.0 copy-done
  224.0 14.6 %fusion.7 = bf16[768,1024]{1,0:T(8,128)(2,1)} fusion(bf16[1,1024,1024]{2,1,0:T(8,128)(2,1)S(1)} %copy-done, bf16[768,4096]{1,0:T(8,128)(2,1)} %bitcast.94, bf16[1,4096,1024]{2,1,0:T(8,128)(2,1)} %param.12), kind=kOutput, calls=%fused_computation.16 | convolution fusion | flops 8055422976 | bytes 18350080 | tf_op jit(solution)/shard_map/dot_general | solution.py:62
  238.6 3.9 %reshape.120 = bf16[8,1,1,96,4,256]{5,4,3,0,2,1:T(4,128)(2,1)} reshape(bf16[768,1024]{1,0:T(8,128)(2,1)} %fusion.7) | data formatting | bytes 3145728 | tf_op jit(solution)/shard_map/reshape | solution.py:66
  242.5 4.4 %all-to-all-start.1 = ((bf16[8,1,1,96,4,256]{5,4,3,2,1,0:T(4,128)(2,1)}), bf16[8,1,1,96,4,256]{5,4,3,2,1,0:T(4,128)(2,1)}, u32[]{:S(2)}, u32[]{:S(2)}) async-start(bf16[8,1,1,96,4,256]{5,4,3,2,1,0:T(4,128)(2,1)} %bitcast.95), calls=%async_computation.2 | async-start | bytes 3145728 | tf_op jit(solution)/shard_map/all_to_all | solution.py:68
  246.9 0.0 reduce-scatter.2.cloned.1.call-start
  247.0 2.6 fusion.23
  249.6 0.0 reduce-scatter.2.cloned.1.call-update
  249.6 0.0 copy-done.2
  249.7 20.5 %reduce-scatter.2.cloned.1.call-done = f32[8,768]{1,0:T(8,128)} async-done(((f32[32,768]{1,0:T(8,128)}), f32[8,768]{1,0:T(8,128)}) %reduce-scatter.2.cloned.1.call-update) | async-done | bytes 24592 | tf_op jit(solution)/shard_map/reduce_scatter | solution.py:34
  270.2 0.8 reduce_max.9
  271.0 0.8 exponential_reduce_fusion
  271.8 0.0 copy-done.1
  271.8 9.4 %gather_fusion.2 = f32[1536]{0:T(1024)S(1)} fusion(f32[8,768]{1,0:T(8,128)S(1)} %copy-done.1, s32[1536]{0:T(1024)S(1)} %reshape.139), kind=kCustom, calls=%fused_computation.2 | custom fusion | bytes 24576 | tf_op jit(solution)/shard_map/jit(take_along_axis)/gather | solution.py:77
  281.2 5.2 %all-gather.3 = f32[4,1,768]{2,1,0:T(1,128)S(1)} all-gather(f32[1,1,768]{2,1,0:T(1,128)S(1)} %reshape.168), channel_id=2, replica_groups=mesh['expert'=8,'gate'=4] {'gate'}, dimensions={0}, use_global_device_ids=true | all-gather | bytes 15360 | tf_op jit(solution)/shard_map/all_gather | solution.py:8
  286.4 5.2 %all-gather.4 = f32[4,1,768]{2,1,0:T(1,128)S(1)} all-gather(f32[1,1,768]{2,1,0:T(1,128)S(1)} %reshape.170), channel_id=3, replica_groups=mesh['expert'=8,'gate'=4] {'gate'}, dimensions={0}, use_global_device_ids=true | all-gather | bytes 15360 | tf_op jit(solution)/shard_map/all_gather | solution.py:8
  291.6 5.2 %all-gather.5 = f32[4,2,768]{2,1,0:T(2,128)S(1)} all-gather(f32[1,2,768]{2,1,0:T(2,128)S(1)} %fusion.19), channel_id=4, replica_groups=mesh['expert'=8,'gate'=4] {'gate'}, dimensions={0}, use_global_device_ids=true | all-gather | bytes 30720 | tf_op jit(solution)/shard_map/all_gather | solution.py:8
  296.8 0.0 all-to-all-done.1
  296.8 2.8 copy.24
  299.7 4.3 %all-to-all-start.2 = ((bf16[1,8,1,96,4,256]{5,3,1,2,0,4:T(8,128)(2,1)}), bf16[1,8,1,96,4,256]{5,3,1,2,0,4:T(8,128)(2,1)}, u32[]{:S(2)}, u32[]{:S(2)}) async-start(bf16[1,8,1,96,4,256]{5,3,1,2,0,4:T(8,128)(2,1)} %copy.24), calls=%async_computation.3 | async-start | bytes 3145728 | tf_op jit(solution)/shard_map/all_to_all | solution.py:67
  304.0 0.3 while.19
  304.4 19.8 %all-to-all-done.2 = bf16[1,8,1,96,4,256]{5,3,1,2,0,4:T(8,128)(2,1)} async-done(((bf16[1,8,1,96,4,256]{5,3,1,2,0,4:T(8,128)(2,1)}), bf16[1,8,1,96,4,256]{5,3,1,2,0,4:T(8,128)(2,1)}, u32[]{:S(2)}, u32[]{:S(2)}) %all-to-all-start.2) | async-done | bytes 1572896 | tf_op jit(solution)/shard_map/all_to_all | solution.py:67
  324.1 2.7 copy.25
  326.8 5.3 %gather_fusion.1 = bf16[1536,256]{1,0:T(8,128)(2,1)S(1)} fusion(bf16[3072,256]{1,0:T(8,128)(2,1)} %bitcast.92, s32[2048]{0:T(1024)S(1)} %pad_clamp_fusion), kind=kCustom, calls=%fused_computation.1 | custom fusion | bytes 1579008 | tf_op jit(solution)/shard_map/gather | solution.py:85
  332.1 1.9 reshape.122
  334.0 3.3 fusion.22
  337.2 1.0 fusion.12
  (38 shorter events, 0.5 us)
Async XLA Ops:
  6.5 217.4 %copy-start = (bf16[1,1024,1024]{2,1,0:T(8,128)(2,1)S(1)}, bf16[1,1024,1024]{2,1,0:T(8,128)(2,1)}, u32[]{:S(2)}) copy-start(bf16[1,1024,1024]{2,1,0:T(8,128)(2,1)} %param.13) | copy-start | bytes 6291460
  6.5 51.5 %all-gather.8.cloned.1.call-start = ((), (), s32[]{:S(2)}) async-start(), calls=%async_computation.5 | async-start | bytes 7864320 | tf_op jit(solution)/shard_map/all_gather | solution.py:50
  238.6 8.4 %copy-start.3 = (bf16[1024,32]{0,1:T(8,128)(2,1)S(1)}, bf16[1024,32]{0,1:T(8,128)(2,1)}, u32[]{:S(2)}) copy-start(bf16[1024,32]{0,1:T(8,128)(2,1)} %param.9) | copy-start | bytes 196612
  242.5 7.1 %copy-start.2 = (s32[768,2]{0,1:T(2,128)S(1)}, s32[768,2]{0,1:T(2,128)}, u32[]{:S(2)}) copy-start(s32[768,2]{0,1:T(2,128)} %param.10) | copy-start | bytes 18436
  242.5 7.2 %copy-start.4 = (s32[768]{0:T(1024)S(1)}, s32[768]{0:T(1024)}, u32[]{:S(2)}) copy-start(s32[768]{0:T(1024)} %param.11) | copy-start | bytes 9220
  242.5 54.3 %all-to-all-start.1 = ((bf16[8,1,1,96,4,256]{5,4,3,2,1,0:T(4,128)(2,1)}), bf16[8,1,1,96,4,256]{5,4,3,2,1,0:T(4,128)(2,1)}, u32[]{:S(2)}, u32[]{:S(2)}) async-start(bf16[8,1,1,96,4,256]{5,4,3,2,1,0:T(4,128)(2,1)} %bitcast.95), calls=%async_computation.2 | async-start | bytes 3145728 | tf_op jit(solution)/shard_map/all_to_all | solution.py:68
  246.9 23.3 %reduce-scatter.2.cloned.1.call-start = ((), (), s32[]{:S(2)}) async-start(), calls=%async_computation.4 | async-start | bytes 122880 | tf_op jit(solution)/shard_map/reduce_scatter | solution.py:34
  270.2 1.6 copy-start.1
  299.7 24.5 %all-to-all-start.2 = ((bf16[1,8,1,96,4,256]{5,3,1,2,0,4:T(8,128)(2,1)}), bf16[1,8,1,96,4,256]{5,3,1,2,0,4:T(8,128)(2,1)}, u32[]{:S(2)}, u32[]{:S(2)}) async-start(bf16[1,8,1,96,4,256]{5,3,1,2,0,4:T(8,128)(2,1)} %copy.24), calls=%async_computation.3 | async-start | bytes 3145728 | tf_op jit(solution)/shard_map/all_to_all | solution.py:67
Sparse Core Ops, SparseCore 0:
  8.9 49.0 all-gather.7
  250.1 19.9 reduce-scatter.1
where the time goes:
time: 346 us; the launch traced here: 345 us
  blocking collectives  160 us (46%)
  waiting for transfers between devices  72.8 us (21%)
  local copies, waits for them, and re-layouts  60 us (17%)
  matrix products  17.2 us (5%)
  between operations  13.7 us (4%)
  other arithmetic  12.8 us (4%)
  starting transfers between devices  8.8 us (3%)
    all_to_all x1, blocking collectives, per_device(): lax.all_to_all(outgoing, 'expert', split_axis=0, concat_axis=0, tiled=True)  144 us
    all_gather x1, waiting for transfers between devices, per_device(): whole_rows = lax.all_gather(samples, 'gate', axis=1, tiled=True)  31.8 us
    reduce_scatter x1, waiting for transfers between devices, per_device(): lax.psum_scatter(lax.dot_general(gate_weight, samples, (((0,), (1,)), (()...  20.5 us
    all_to_all x1, waiting for transfers between devices, per_device(): lax.all_to_all(lax.all_to_all(outbound, 'expert', split_axis=0, concat_ax...  19.8 us
    all_gather x3, blocking collectives, joined(): everything = jax.tree.map(lambda part: lax.all_gather(part, axis), shard)  15.6 us
    gather x1, local copies, waits for them, and re-layouts, per_device(): outgoing = padded[column_owners]  15.6 us
    dot_general x1, matrix products, per_device(): jnp.dot(active, down_weight[0], preferred_element_type=jnp.float32)  14.6 us
    gather x3, local copies, waits for them, and re-layouts, per_device(): jnp.take_along_axis(logits_t, jnp.clip(offset, 0, col_count - 1).T, axis=0)  9.39 us
  transfers between devices with their start and end apart: 4, of which 3 were waited for; matrix products, arithmetic and copies ran while one was open for 9% of the time, Pallas kernels for 0%

commit v1 on v0

--- a/solution.py
+++ b/solution.py
@@ -47,7 +47,7 @@
     position = flat_ids * capacity + slot_rank
     row_index = jnp.repeat(jnp.arange(row_count, dtype=jnp.int32), 2)
     owners = jnp.full((expert_count * capacity,), row_count, jnp.int32).at[position].set(row_index)
-    whole_rows = lax.all_gather(samples, "gate", axis=1, tiled=True)
+    whole_rows = jnp.concatenate(lax.all_gather(samples, axis_name="gate"), 1)
     padded = jnp.concatenate(
         [whole_rows, jnp.zeros((1, whole_rows.shape[1]), whole_rows.dtype)], axis=0
     )

time: 346 us -> 360 us (1.040)
  local copies, waits for them, and re-layouts: 60 us -> 74.4 us
    all_gather x0 -> x1, local copies, waits for them, and re-layouts: none -> 10.3 us  [per_device(): whole_rows = jnp.concatenate(lax.all_gather(samples, axis_name='gate'), 1)]
    unnamed x15 -> x16, local copies, waits for them, and re-layouts: 0.9 us -> 7.79 us
where the time goes in v1:
time: 360 us; the launch traced here: 359 us
  blocking collectives  160 us (44%)
  local copies, waits for them, and re-layouts  74.4 us (21%)
  waiting for transfers between devices  72.3 us (20%)
  matrix products  17.2 us (5%)
  between operations  13.7 us (4%)
  other arithmetic  12.8 us (4%)
  starting transfers between devices  9.06 us (3%)
    all_to_all x1, blocking collectives, per_device(): lax.all_to_all(outgoing, 'expert', split_axis=0, concat_axis=0, tiled=True)  144 us
    all_gather x1, waiting for transfers between devices, per_device(): whole_rows = jnp.concatenate(lax.all_gather(samples, axis_name='gate'), 1)  31.6 us
    reduce_scatter x1, waiting for transfers between devices, per_device(): lax.psum_scatter(lax.dot_general(gate_weight, samples, (((0,), (1,)), (()...  20.5 us
    all_to_all x1, waiting for transfers between devices, per_device(): lax.all_to_all(lax.all_to_all(outbound, 'expert', split_axis=0, concat_ax...  19.5 us
    gather x1, local copies, waits for them, and re-layouts, per_device(): outgoing = padded[column_owners]  15.8 us
    all_gather x3, blocking collectives, joined(): everything = jax.tree.map(lambda part: lax.all_gather(part, axis), shard)  15.6 us
    dot_general x1, matrix products, per_device(): jnp.dot(active, down_weight[0], preferred_element_type=jnp.float32)  14.6 us
    all_gather x1, local copies, waits for them, and re-layouts, per_device(): whole_rows = jnp.concatenate(lax.all_gather(samples, axis_name='gate'), 1)  10.3 us
  transfers between devices with their start and end apart: 4, of which 3 were waited for; matrix products, arithmetic and copies ran while one was open for 9% of the time, Pallas kernels for 0%

profile of v1, /device:TPU:0, one launch (start us, length us, event | category | flops | bytes accessed | tf_op | source)
XLA Modules:
  0.0 359.3 jit_solution(8279300484511642544)
XLA Ops:
  6.5 0.0 copy-start
  6.5 0.0 all-gather.9.cloned.1.call-start
  6.5 0.7 all-gather.9.cloned.1.call-update
  7.3 0.9 copy.22
  8.1 0.2 eq.29
  8.4 0.2 eq.25
  8.6 0.7 broadcast_multiply_fusion
  9.3 0.2 copy.21
  9.5 0.3 mul.137
  9.8 9.1 %reduce-window.6 = s32[32,12,128]{2,1,0:T(8,128)S(1)} reduce-window(s32[32,12,128]{2,1,0:T(8,128)S(1)} %fusion.14, s32[]{:T(128)} %constant.77.clone.1), window={size=1x1x128 pad=0_0x0_0x127_0}, to_apply=%region_5.6 | reduce-window | flops 6242304 | bytes 393220 | tf_op jit(solution)/shard_map/reduce-window
  18.8 0.1 slice.52
  19.0 0.2 copy.24
  19.2 0.1 copy.25
  19.3 0.2 reshape.157
  19.6 0.1 add_add_fusion
  19.7 0.1 fusion.16
  19.8 6.4 %scatter_custom_fusion = s32[3072]{0:T(1024)S(1)} fusion(s32[1536]{0:T(1024)S(1)} %fusion.17, s32[1536]{0:T(1024)S(1)} %reshape.157, s32[]{:T(128)} %constant.86.clone.1), kind=kCustom, calls=%fused_computation.44 | custom fusion | bytes 12292 | tf_op jit(solution)/shard_map/scatter | solution.py:49
  26.2 0.1 reshape.126
  26.3 0.1 reshape.133
  26.4 31.6 %all-gather.9.cloned.1.call-done = bf16[3072,1024]{1,0:T(8,128)(2,1)} async-done(((bf16[768,1024]{1,0:T(8,128)(2,1)}), bf16[3072,1024]{1,0:T(8,128)(2,1)}) %all-gather.9.cloned.1.call-update) | async-done | bytes 6291472 | tf_op jit(solution)/shard_map/all_gather | solution.py:50
  58.0 10.3 %copy.20 = bf16[4,768,1024]{2,0,1:T(4,128)(2,1)} copy(bf16[4,768,1024]{2,1,0:T(8,128)(2,1)} %bitcast.100) | data formatting | bytes 12582912 | tf_op jit(solution)/shard_map/all_gather | solution.py:50
  68.3 6.9 %copy.35 = bf16[96,8,4,1024]{3,1,2,0:T(8,128)(2,1)S(1)} copy(bf16[96,8,4,1024]{3,2,1,0:T(4,128)(2,1)} %bitcast.99) | data formatting | bytes 12582912
  75.2 3.1 concatenate.3
  78.3 15.8 %gather_fusion = bf16[768,4096]{1,0:T(8,128)(2,1)} fusion(bf16[769,4096]{1,0:T(8,128)(2,1)} %concatenate.3, s32[1024]{0:T(1024)S(1)} %pad_clamp_fusion.1), kind=kCustom, calls=%fused_computation | custom fusion | bytes 12585984 | tf_op jit(solution)/shard_map/gather | solution.py:57
  94.1 144.1 %all_to_all.32 = bf16[8,96,4096]{2,1,0:T(8,128)(2,1)} all-to-all(bf16[8,96,4096]{2,1,0:T(8,128)(2,1)} %bitcast.98), channel_id=1, replica_groups=mesh['expert'=8,'gate'=4] {'expert'}, dimensions={0} | all-to-all | bytes 12582912 | tf_op jit(solution)/shard_map/all_to_all | solution.py:58
  238.2 14.6 %fusion.7 = bf16[768,1024]{1,0:T(8,128)(2,1)} fusion(bf16[1,1024,1024]{2,1,0:T(8,128)(2,1)S(1)} %copy-done, bf16[768,4096]{1,0:T(8,128)(2,1)} %bitcast.101, bf16[1,4096,1024]{2,1,0:T(8,128)(2,1)} %param.12), kind=kOutput, calls=%fused_computation.16 | convolution fusion | flops 8055422976 | bytes 18350080 | tf_op jit(solution)/shard_map/dot_general | solution.py:62
  252.8 3.9 %reshape.128 = bf16[8,1,1,96,4,256]{5,4,3,0,2,1:T(4,128)(2,1)} reshape(bf16[768,1024]{1,0:T(8,128)(2,1)} %fusion.7) | data formatting | bytes 3145728 | tf_op jit(solution)/shard_map/reshape | solution.py:66
  256.7 4.4 %all-to-all-start.1 = ((bf16[8,1,1,96,4,256]{5,4,3,2,1,0:T(4,128)(2,1)}), bf16[8,1,1,96,4,256]{5,4,3,2,1,0:T(4,128)(2,1)}, u32[]{:S(2)}, u32[]{:S(2)}) async-start(bf16[8,1,1,96,4,256]{5,4,3,2,1,0:T(4,128)(2,1)} %bitcast.102), calls=%async_computation.2 | async-start | bytes 3145728 | tf_op jit(solution)/shard_map/all_to_all | solution.py:68
  261.2 0.0 reduce-scatter.2.cloned.1.call-start
  261.2 2.6 fusion.23
  263.8 0.0 reduce-scatter.2.cloned.1.call-update
  264.0 20.5 %reduce-scatter.2.cloned.1.call-done = f32[8,768]{1,0:T(8,128)} async-done(((f32[32,768]{1,0:T(8,128)}), f32[8,768]{1,0:T(8,128)}) %reduce-scatter.2.cloned.1.call-update) | async-done | bytes 24592 | tf_op jit(solution)/shard_map/reduce_scatter | solution.py:34
  284.4 0.8 reduce_max.9
  285.2 0.8 exponential_reduce_fusion
  286.0 9.4 %gather_fusion.2 = f32[1536]{0:T(1024)S(1)} fusion(f32[8,768]{1,0:T(8,128)S(1)} %copy-done.1, s32[1536]{0:T(1024)S(1)} %reshape.147), kind=kCustom, calls=%fused_computation.2 | custom fusion | bytes 24576 | tf_op jit(solution)/shard_map/jit(take_along_axis)/gather | solution.py:77
  295.4 5.2 %all-gather.4 = f32[4,1,768]{2,1,0:T(1,128)S(1)} all-gather(f32[1,1,768]{2,1,0:T(1,128)S(1)} %reshape.177), channel_id=2, replica_groups=mesh['expert'=8,'gate'=4] {'gate'}, dimensions={0}, use_global_device_ids=true | all-gather | bytes 15360 | tf_op jit(solution)/shard_map/all_gather | solution.py:8
  300.6 5.2 %all-gather.5 = f32[4,1,768]{2,1,0:T(1,128)S(1)} all-gather(f32[1,1,768]{2,1,0:T(1,128)S(1)} %reshape.179), channel_id=3, replica_groups=mesh['expert'=8,'gate'=4] {'gate'}, dimensions={0}, use_global_device_ids=true | all-gather | bytes 15360 | tf_op jit(solution)/shard_map/all_gather | solution.py:8
  305.8 5.2 %all-gather.6 = f32[4,2,768]{2,1,0:T(2,128)S(1)} all-gather(f32[1,2,768]{2,1,0:T(2,128)S(1)} %fusion.19), channel_id=4, replica_groups=mesh['expert'=8,'gate'=4] {'gate'}, dimensions={0}, use_global_device_ids=true | all-gather | bytes 30720 | tf_op jit(solution)/shard_map/all_gather | solution.py:8
  311.1 0.0 all-to-all-done.1
  311.1 2.8 copy.27
  313.9 4.6 %all-to-all-start.2 = ((bf16[1,8,1,96,4,256]{5,3,1,2,0,4:T(8,128)(2,1)}), bf16[1,8,1,96,4,256]{5,3,1,2,0,4:T(8,128)(2,1)}, u32[]{:S(2)}, u32[]{:S(2)}) async-start(bf16[1,8,1,96,4,256]{5,3,1,2,0,4:T(8,128)(2,1)} %copy.27), calls=%async_computation.3 | async-start | bytes 3145728 | tf_op jit(solution)/shard_map/all_to_all | solution.py:67
  318.5 0.3 while.19
  318.9 19.5 %all-to-all-done.2 = bf16[1,8,1,96,4,256]{5,3,1,2,0,4:T(8,128)(2,1)} async-done(((bf16[1,8,1,96,4,256]{5,3,1,2,0,4:T(8,128)(2,1)}), bf16[1,8,1,96,4,256]{5,3,1,2,0,4:T(8,128)(2,1)}, u32[]{:S(2)}, u32[]{:S(2)}) %all-to-all-start.2) | async-done | bytes 1572896 | tf_op jit(solution)/shard_map/all_to_all | solution.py:67
  338.4 2.7 copy.28
  341.0 5.3 %gather_fusion.1 = bf16[1536,256]{1,0:T(8,128)(2,1)S(1)} fusion(bf16[3072,256]{1,0:T(8,128)(2,1)} %bitcast.96, s32[2048]{0:T(1024)S(1)} %pad_clamp_fusion), kind=kCustom, calls=%fused_computation.1 | custom fusion | bytes 1579008 | tf_op jit(solution)/shard_map/gather | solution.py:85
  346.3 1.9 reshape.130
  348.2 3.3 fusion.22
  351.5 1.0 fusion.12
  (40 shorter events, 0.5 us)
Async XLA Ops:
  6.5 231.7 %copy-start = (bf16[1,1024,1024]{2,1,0:T(8,128)(2,1)S(1)}, bf16[1,1024,1024]{2,1,0:T(8,128)(2,1)}, u32[]{:S(2)}) copy-start(bf16[1,1024,1024]{2,1,0:T(8,128)(2,1)} %param.13) | copy-start | bytes 6291460
  6.5 51.5 %all-gather.9.cloned.1.call-start = ((), (), s32[]{:S(2)}) async-start(), calls=%async_computation.5 | async-start | bytes 7864320 | tf_op jit(solution)/shard_map/all_gather | solution.py:50
  252.8 8.4 %copy-start.3 = (bf16[1024,32]{0,1:T(8,128)(2,1)S(1)}, bf16[1024,32]{0,1:T(8,128)(2,1)}, u32[]{:S(2)}) copy-start(bf16[1024,32]{0,1:T(8,128)(2,1)} %param.9) | copy-start | bytes 196612
  256.7 7.1 %copy-start.2 = (s32[768,2]{0,1:T(2,128)S(1)}, s32[768,2]{0,1:T(2,128)}, u32[]{:S(2)}) copy-start(s32[768,2]{0,1:T(2,128)} %param.10) | copy-start | bytes 18436
  256.7 7.2 %copy-start.4 = (s32[768]{0:T(1024)S(1)}, s32[768]{0:T(1024)}, u32[]{:S(2)}) copy-start(s32[768]{0:T(1024)} %param.11) | copy-start | bytes 9220
  256.7 54.3 %all-to-all-start.1 = ((bf16[8,1,1,96,4,256]{5,4,3,2,1,0:T(4,128)(2,1)}), bf16[8,1,1,96,4,256]{5,4,3,2,1,0:T(4,128)(2,1)}, u32[]{:S(2)}, u32[]{:S(2)}) async-start(bf16[8,1,1,96,4,256]{5,4,3,2,1,0:T(4,128)(2,1)} %bitcast.102), calls=%async_computation.2 | async-start | bytes 3145728 | tf_op jit(solution)/shard_map/all_to_all | solution.py:68
  261.2 23.3 %reduce-scatter.2.cloned.1.call-start = ((), (), s32[]{:S(2)}) async-start(), calls=%async_computation.4 | async-start | bytes 122880 | tf_op jit(solution)/shard_map/reduce_scatter | solution.py:34
  284.4 1.6 copy-start.1
  313.9 24.5 %all-to-all-start.2 = ((bf16[1,8,1,96,4,256]{5,3,1,2,0,4:T(8,128)(2,1)}), bf16[1,8,1,96,4,256]{5,3,1,2,0,4:T(8,128)(2,1)}, u32[]{:S(2)}, u32[]{:S(2)}) async-start(bf16[1,8,1,96,4,256]{5,3,1,2,0,4:T(8,128)(2,1)} %copy.27), calls=%async_computation.3 | async-start | bytes 3145728 | tf_op jit(solution)/shard_map/all_to_all | solution.py:67
Sparse Core Ops, SparseCore 0:
  8.9 49.0 all-gather.8
  264.4 19.9 reduce-scatter.1
